TPU v7x, 32 devices: a whole 2x2x4 slice. The times are simulated.
32 devices in a mesh: gx: 8 (over y, x, core), gy: 4 (over z).
Axes of the slice: x: 2, y: 2, z: 4, core: 2. Of those that a mesh axis runs over, the one named last changes fastest.
Arguments:
- probes: float32 [16, 128, 128, 256], P(None, 'gx', 'gy'), may hold values from -6 to 6
- diffusivity: float32 [128, 128, 256], P('gx', 'gy'), may hold values from 0.5 to 2
- wind_speed: float32 [3], replicated, may hold values from 0.5 to 2
- sensor_cell: int32 [8, 4, 128], P('gx', 'gy'), may hold values from 0 to 131071
- sensor_owner: int32 [8, 4, 128, 1], P('gx', 'gy'), may hold values from 0 to 31; in each aligned block of 128 rows (0 to 127, 128 to 255, ..., all dimensions but the last counted through in order) at most 4 rows name the same one
- sensor_count: int32 [8, 4], P('gx', 'gy'), may hold values from 64 to 128
- goal_weight: float32 [8, 4, 128, 16], P('gx', 'gy'), may hold values from -0.6 to 0.6
Outputs:
- fields: float32 [16, 128, 128, 256], P(None, 'gx', 'gy')
- goal_block: float32 [512, 16], P(('gx', 'gy'))
- ritz_gram: float32 [16, 16], replicated
Inputs may be any that keep to these rules, and one draw needn't show every extreme that they name: `sensor_owner`: among the rows of one device, no owner is named more than 4 times, a bound that some block reaches.
All inputs are finite; a program needn't handle non-finite values.
Results may differ from a plain program's by a relative error of at most 0.0003.
Values sent between devices are 32-bit elements; how exact they have to be, the bound alone decides.
A program may use at most 192 MiB of HBM per device.

v0:
```python
import jax
import jax.numpy as jnp
from jax import lax
from jax.experimental import pallas as pl
from jax.experimental.pallas import tpu as pltpu
from jax.sharding import PartitionSpec as P

STEPS = 2
SWEEPS = 4

time_step = 2.0

LANES = 8
CHUNK = 4


def schedule():
    plan, read = [], 0
    for _ in range(STEPS):
        source = read
        others = [b for b in range(3) if b != source]
        for k in range(SWEEPS):
            written = others[k % 2]
            plan.append((read, source, written))
            read = written
    return plan


def sweeps_kernel(wind, field, inverse, mixing, out, held0, held1, held2, inv, mix, load_sem, store_sem, send_sem, recv_sem):
    held = (held0, held1, held2)
    groups, nx, ny = field.shape[0], field.shape[1], field.shape[2]
    nz = field.shape[4]
    gx, gy = lax.axis_index("gx"), lax.axis_index("gy")
    n_gx, n_gy = lax.axis_size("gx"), lax.axis_size("gy")
    xs, ys = pl.ds(1, nx), pl.ds(1, ny)

    loads = [pltpu.make_async_copy(field.at[g], held[0].at[g, xs, ys], load_sem.at[g]) for g in range(groups)]
    loads.append(pltpu.make_async_copy(inverse, inv, load_sem.at[groups]))
    loads.append(pltpu.make_async_copy(mixing, mix, load_sem.at[groups + 1]))
    for copy in loads:
        copy.start()

    row = jnp.zeros((ny + 2, LANES, nz), jnp.float32)
    for b in range(3):
        for g in range(groups):
            held[b][g, 0] = row
            held[b][g, nx + 1] = row
            held[b][g, xs, 0] = row[:nx] if nx <= ny + 2 else jnp.zeros((nx, LANES, nz), jnp.float32)
            held[b][g, xs, ny + 1] = row[:nx] if nx <= ny + 2 else jnp.zeros((nx, LANES, nz), jnp.float32)

    routes = (
        (gx < n_gx - 1, gx > 0, (gx + 1, gy)),
        (gx > 0, gx < n_gx - 1, (gx - 1, gy)),
        (gy < n_gy - 1, gy > 0, (gx, gy + 1)),
        (gy > 0, gy < n_gy - 1, (gx, gy - 1)),
    )
    barrier = pltpu.get_barrier_semaphore()
    for there, _, target in routes:
        @pl.when(there)
        def _():
            pl.semaphore_signal(barrier, inc=1, device_id=target, device_id_type=pl.DeviceIdType.MESH)
    peers = sum(there.astype(jnp.int32) for there, _, _ in routes)
    pl.semaphore_wait(barrier, peers)

    def face(d, b, g, turn):
        if d == 0:
            src, dst = held[b].at[g, nx, ys], held[b].at[g, 0, ys]
        elif d == 1:
            src, dst = held[b].at[g, 1, ys], held[b].at[g, nx + 1, ys]
        elif d == 2:
            src, dst = held[b].at[g, xs, ny], held[b].at[g, xs, 0]
        else:
            src, dst = held[b].at[g, xs, 1], held[b].at[g, xs, ny + 1]
        return pltpu.make_async_remote_copy(
            src_ref=src,
            dst_ref=dst,
            send_sem=send_sem.at[turn % 2, g, d],
            recv_sem=recv_sem.at[turn % 2, g, d],
            device_id=routes[d][2],
            device_id_type=pl.DeviceIdType.MESH,
        )

    def start(d, b, g, turn):
        @pl.when(routes[d][0])
        def _():
            face(d, b, g, turn).start()

    def wait_send(d, b, g, turn):
        @pl.when(routes[d][0])
        def _():
            face(d, b, g, turn).wait_send()

    def wait_recv(d, b, g, turn):
        @pl.when(routes[d][1])
        def _():
            face(d, b, g, turn).wait_recv()

    w0, w1, w2 = wind[0], wind[1], wind[2]
    lane = lax.broadcasted_iota(jnp.int32, (CHUNK, LANES, nz), 2)

    def plane(x, g, read, source, written):
        for y in range(1, ny + 1, CHUNK):
            centre = held[read][g, x, pl.ds(y, CHUNK)]
            x_low = held[read][g, x - 1, pl.ds(y, CHUNK)]
            x_high = held[read][g, x + 1, pl.ds(y, CHUNK)]
            y_low = held[read][g, x, pl.ds(y - 1, CHUNK)]
            y_high = held[read][g, x, pl.ds(y + 1, CHUNK)]
            z_low = jnp.where(lane == 0, 0.0, pltpu.roll(centre, 1, 2))
            z_high = jnp.where(lane == nz - 1, 0.0, pltpu.roll(centre, nz - 1, 2))
            beside = (x_low + x_high) + (y_low + y_high) + (z_low + z_high)
            upwind = w0 * x_low + w1 * y_low + w2 * z_low
            start_value = held[source][g, x, pl.ds(y, CHUNK)]
            r = inv[x - 1, pl.ds(y - 1, CHUNK)]
            a = mix[x - 1, pl.ds(y - 1, CHUNK)]
            held[written][g, x, pl.ds(y, CHUNK)] = (start_value + upwind) * r + a * beside

    plan = schedule()
    last = len(plan)
    for g in range(groups):
        loads[g].wait()
        for d in range(4):
            start(d, 0, g, 0)
    loads[groups].wait()
    loads[groups + 1].wait()

    stores = []
    for turn, (read, source, written) in enumerate(plan, 1):
        for g in range(groups):
            for d in range(4):
                wait_recv(d, read, g, turn - 1)
                if turn >= 2:
                    wait_send(d, plan[turn - 3][2] if turn >= 3 else 0, g, turn - 2)
            def end(i, carry):
                plane(1 + i * (nx - 1), g, read, source, written)
                return carry

            lax.fori_loop(0, 2, end, 0)
            if turn < last:
                for d in (0, 1):
                    start(d, written, g, turn)

            def inner(x, carry):
                plane(x, g, read, source, written)
                return carry

            lax.fori_loop(2, nx, inner, 0)
            if turn < last:
                for d in (2, 3):
                    start(d, written, g, turn)
            else:
                stores.append(pltpu.make_async_copy(held[written].at[g, xs, ys], out.at[g], store_sem.at[g]))
                stores[-1].start()
    for g in range(groups):
        for d in range(4):
            wait_send(d, plan[last - 1][0], g, last - 1)
        stores[g].wait()


def run_sweeps(wind, field, inverse, mixing):
    groups, nx, ny, _, nz = field.shape
    hbm = pl.BlockSpec(memory_space=pl.ANY)
    return pl.pallas_call(
        sweeps_kernel,
        out_shape=jax.ShapeDtypeStruct(field.shape, jnp.float32),
        in_specs=[pl.BlockSpec(memory_space=pltpu.SMEM), hbm, hbm, hbm],
        out_specs=hbm,
        scratch_shapes=[
            *[pltpu.VMEM((groups, nx + 2, ny + 2, LANES, nz), jnp.float32)] * 3,
            pltpu.VMEM((nx, ny, LANES, nz), jnp.float32),
            pltpu.VMEM((nx, ny, LANES, nz), jnp.float32),
            pltpu.SemaphoreType.DMA((groups + 2,)),
            pltpu.SemaphoreType.DMA((groups,)),
            pltpu.SemaphoreType.DMA((2, groups, 4)),
            pltpu.SemaphoreType.DMA((2, groups, 4)),
        ],
        compiler_params=pltpu.CompilerParams(
            collective_id=0, has_side_effects=True, vmem_limit_bytes=60 * 1024 * 1024
        ),
    )(wind, field, inverse, mixing)


def gather_kernel(payload, out, send_sem, recv_sem):
    n_gy = lax.axis_size("gy")
    devices = lax.axis_size("gx") * n_gy
    me = lax.axis_index("gx") * n_gy + lax.axis_index("gy")

    def place(k):
        other = (me + k) % devices
        return (other // n_gy, other % n_gy)

    def greet(k, carry):
        pl.semaphore_signal(
            pltpu.get_barrier_semaphore(), inc=1, device_id=place(k), device_id_type=pl.DeviceIdType.MESH
        )
        return carry

    lax.fori_loop(1, devices, greet, 0)
    pl.semaphore_wait(pltpu.get_barrier_semaphore(), devices - 1)

    def copy(k, slot):
        return pltpu.make_async_remote_copy(
            src_ref=payload,
            dst_ref=out.at[slot],
            send_sem=send_sem.at[k],
            recv_sem=recv_sem.at[k],
            device_id=place(k),
            device_id_type=pl.DeviceIdType.MESH,
        )

    def send(k, carry):
        copy(k, me).start()
        return carry

    def finish(k, carry):
        arriving = copy(k, (me + devices - k) % devices)
        arriving.wait_send()
        arriving.wait_recv()
        return carry

    lax.fori_loop(1, devices, send, 0)
    out[me] = payload[...]
    lax.fori_loop(1, devices, finish, 0)


def gather_all(payload):
    devices = lax.axis_size("gx") * lax.axis_size("gy")
    vmem = pl.BlockSpec(memory_space=pltpu.VMEM)
    return pl.pallas_call(
        gather_kernel,
        out_shape=jax.ShapeDtypeStruct((devices,) + payload.shape, jnp.float32),
        in_specs=[vmem],
        out_specs=vmem,
        scratch_shapes=[pltpu.SemaphoreType.DMA((devices,)), pltpu.SemaphoreType.DMA((devices,))],
        compiler_params=pltpu.CompilerParams(collective_id=1, has_side_effects=True),
    )(payload)


def body(probes, diffusivity, wind_speed, sensor_cell, sensor_owner, sensor_count, goal_weight):
    probe_count, nx, ny, nz = probes.shape
    groups = probe_count // LANES
    field = probes.reshape(groups, LANES, nx, ny, nz).transpose(0, 2, 3, 1, 4)
    inverse = 1.0 / (
        1.0 + time_step * (6.0 * diffusivity + wind_speed[0] + wind_speed[1] + wind_speed[2])
    )
    mixing = time_step * diffusivity * inverse
    wide = (nx, ny, LANES, nz)
    state = run_sweeps(
        time_step * wind_speed,
        field,
        jnp.broadcast_to(inverse[:, :, None, :], wide),
        jnp.broadcast_to(mixing[:, :, None, :], wide),
    )
    fields = state.transpose(0, 3, 1, 2, 4).reshape(probes.shape)

    sensor_rows = sensor_cell.shape[2]
    goal_count = goal_weight.shape[3]
    device_count = lax.axis_size("gx") * lax.axis_size("gy")
    cells = sensor_cell.reshape(-1)
    columns = jnp.take(state.reshape(groups, nx * ny, LANES, nz), cells // nz, axis=1, mode="clip")
    here = jnp.arange(nz, dtype=jnp.int32)[None, :] == (cells % nz)[:, None]
    readings = jnp.sum(jnp.where(here[None, :, None, :], columns, 0.0), axis=3)
    readings = readings.transpose(1, 0, 2).reshape(sensor_rows, probe_count)
    active = jnp.arange(sensor_rows, dtype=jnp.int32) < sensor_count.reshape(())
    readings = jnp.where(active[:, None], readings, 0.0)
    payload = jnp.concatenate(
        [
            readings,
            goal_weight.reshape(sensor_rows, goal_count),
            sensor_owner.reshape(sensor_rows, 1).astype(jnp.float32),
        ],
        axis=1,
    )
    width = payload.shape[1]
    payload = jnp.pad(payload.T, ((0, -width % 8), (0, 0)))
    everyone = gather_all(payload).transpose(0, 2, 1).reshape(device_count * sensor_rows, -1)
    all_readings = everyone[:, :probe_count]
    all_weights = everyone[:, probe_count : probe_count + goal_count]
    owners = everyone[:, probe_count + goal_count].astype(jnp.int32)
    onehot = (owners[:, None] == jnp.arange(device_count, dtype=jnp.int32)[None, :]).astype(jnp.float32)
    outer = (all_weights[:, :, None] * all_readings[:, None, :]).reshape(-1, goal_count * probe_count)
    goals = jnp.dot(onehot.T, outer, precision=lax.Precision.HIGHEST)
    goals = goals.reshape(device_count * goal_count, probe_count)
    ritz_gram = jnp.dot(goals.T, goals, precision=lax.Precision.HIGHEST)
    mine = lax.axis_index("gx") * lax.axis_size("gy") + lax.axis_index("gy")
    goal_block = lax.dynamic_slice_in_dim(goals, mine * goal_count, goal_count, axis=0)
    return (fields, goal_block, ritz_gram)


def solution(mesh):
    placed = (
        P(None, "gx", "gy", None),
        P("gx", "gy", None),
        P(),
        P("gx", "gy", None),
        P("gx", "gy", None, None),
        P("gx", "gy"),
        P("gx", "gy", None, None),
    )
    return jax.shard_map(
        body,
        mesh=mesh,
        in_specs=placed,
        out_specs=(P(None, "gx", "gy", None), P(("gx", "gy"), None), P()),
        check_vma=False,
    )
```

profile of v0, /device:TPU:0, one launch (start us, length us, event | category | flops | bytes accessed | tf_op | source)
XLA Modules:
  0.0 168.0 jit_solution(12108280021946354981)
XLA Ops:
  0.6 1.4 fusion.5
  2.0 3.1 %multiply_multiply_fusion = (f32[16,32,256]{2,1,0:T(8,128)S(1)}, f32[16,32,256]{2,1,0:T(8,128)S(1)}) fusion(f32[16,32,256]{2,1,0:T(8,128)} %param.8, f32[]{:T(128)} %bitcast.4, f32[]{:T(128)} %bitcast.3, f32[]{:T(128)} %bitcast.2), kind=kLoop, calls=%fused_computation.6 | loop fusion | flops 1179648 | bytes 1572876 | tf_op jit(solution)/shard_map/mul | solution.py:245
  5.1 0.0 copy-start
  5.1 2.4 %broadcast_in_dim.30.inverse = f32[16,32,8,256]{3,2,1,0:T(8,128)} broadcast(f32[16,32,256]{2,1,0:T(8,128)S(1)} %get-tuple-element.6), dimensions={0,1,3} | broadcast | bytes 4718592 | tf_op jit(solution)/shard_map/broadcast_in_dim | solution.py:250
  7.6 2.4 %broadcast_in_dim.31.mixing = f32[16,32,8,256]{3,2,1,0:T(8,128)} broadcast(f32[16,32,256]{2,1,0:T(8,128)S(1)} %get-tuple-element.5), dimensions={0,1,3} | broadcast | bytes 4718592 | tf_op jit(solution)/shard_map/broadcast_in_dim | solution.py:251
  10.0 1.5 copy-done
  11.5 0.0 copy-start.2
  11.6 11.0 %copy.24 = f32[2,8,16,32,256]{4,1,3,2,0:T(8,128)} copy(f32[2,8,16,32,256]{4,3,2,1,0:T(8,128)S(1)} %bitcast.48) | data formatting | bytes 16777216 | tf_op jit(solution)/shard_map/reshape | solution.py:241
  22.5 0.0 copy-done.2
  22.5 0.5 broadcast_multiply_fusion.1.wind
  23.0 0.0 copy-start.3
  23.0 93.1 %shard_map.94 = f32[2,16,32,8,256]{4,3,2,1,0:T(8,128)} custom-call(f32[3]{0:T(128)} %broadcast_multiply_fusion.1.wind, f32[2,16,32,8,256]{4,3,2,1,0:T(8,128)} %bitcast.46, f32[16,32,8,256]{3,2,1,0:T(8,128)} %broadcast_in_dim.30.inverse, f32[16,32,8,256]{3,2,1,0:T(8,128)} %broadcast_in_dim.31.mixing), custom_call_target="tpu_custom_call" | custom-call | tf_op jit(solution)/shard_map/pallas_call | solution.py:162
  116.2 0.0 copy-start.4
  116.2 0.0 copy-start.1
  116.2 0.0 copy-done.3
  116.2 4.1 %gather_fusion = f32[128,2,8,256]{3,2,1,0:T(8,128)S(1)} fusion(f32[2,512,8,256]{3,2,1,0:T(8,128)} %bitcast.44, s32[1024]{0:T(1024)S(1)} %pad_clamp_fusion), kind=kCustom, calls=%fused_computation | custom fusion | bytes 4194816 | tf_op jit(solution)/shard_map/jit(_take)/gather | solution.py:259
  120.3 0.1 iota_compare_fusion.2
  120.4 0.5 select_reduce_fusion
  120.9 0.1 copy.19
  121.7 0.0 copy-done.4
  121.7 0.0 copy-done.1
  121.7 0.6 pad.4.payload
  122.3 30.6 %shard_map.95 = f32[32,40,128]{2,1,0:T(8,128)} custom-call(f32[40,128]{1,0:T(8,128)} %pad.4.payload), custom_call_target="tpu_custom_call" | custom-call | tf_op jit(solution)/shard_map/pallas_call | solution.py:228
  152.9 1.1 copy_bitcast_fusion.1
  154.1 0.5 broadcast_multiply_fusion
  154.6 2.2 %fusion = f32[32,256]{1,0:T(8,128)S(1)} fusion(f32[4096,256]{0,1:T(8,128)S(1)} %bitcast.47, s32[4096]{0:T(1024)S(1)} %bitcast.50), kind=kOutput, calls=%fused_computation.8 | convolution fusion | flops 402784256 | bytes 4243456 | tf_op jit(solution)/shard_map/dot_general | solution.py:281
  156.8 0.1 reshape.179
  156.9 0.6 constant_dynamic-slice_fusion
  157.6 1.2 fusion.6
  158.7 9.3 %copy.18 = f32[2,8,16,32,256]{4,3,2,1,0:T(8,128)} copy(f32[2,8,16,32,256]{4,1,3,2,0:T(8,128)} %bitcast.45) | data formatting | bytes 16777216 | tf_op jit(solution)/shard_map/transpose | solution.py:253
  (9 shorter events, 0.1 us)
Async XLA Ops:
  5.1 6.4 %copy-start = (f32[16,16,32,256]{3,2,1,0:T(8,128)S(1)}, f32[16,16,32,256]{3,2,1,0:T(8,128)}, u32[]{:S(2)}) copy-start(f32[16,16,32,256]{3,2,1,0:T(8,128)} %param.7) | copy-start | bytes 25165828
  11.5 11.0 %copy-start.2 = (f32[3]{0:T(128)S(1)}, f32[3]{0:T(128)}, u32[]{:S(2)}) copy-start(f32[3]{0:T(128)} %param.9) | copy-start | bytes 40
  23.0 93.2 %copy-start.3 = (s32[1,1,128]{2,1,0:T(1,128)S(1)}, s32[1,1,128]{2,1,0:T(1,128)}, u32[]{:S(2)}) copy-start(s32[1,1,128]{2,1,0:T(1,128)} %param.10) | copy-start | bytes 1540
  116.2 5.5 %copy-start.4 = (s32[1,1,128,1]{2,3,1,0:T(1,128)S(1)}, s32[1,1,128,1]{2,3,1,0:T(1,128)}, u32[]{:S(2)}) copy-start(s32[1,1,128,1]{2,3,1,0:T(1,128)} %param.11) | copy-start | bytes 1540
  116.2 5.5 %copy-start.1 = (f32[1,1,128,16]{2,3,1,0:T(8,128)S(1)}, f32[1,1,128,16]{2,3,1,0:T(8,128)}, u32[]{:S(2)}) copy-start(f32[1,1,128,16]{2,3,1,0:T(8,128)} %param.13) | copy-start | bytes 24580
where the time goes:
time: 168 us
  Pallas kernels  124 us (74%)
  local copies, waits for them, and re-layouts  34.6 us (21%)
  other arithmetic  4.75 us (3%)
  matrix products  3.36 us (2%)
    pallas_call x1, Pallas kernels, run_sweeps(): pl.pallas_call(sweeps_kernel, out_shape=jax.ShapeDtypeStruct(field.shape,...  93.1 us
    pallas_call x1, Pallas kernels, gather_all(): pl.pallas_call(gather_kernel, out_shape=jax.ShapeDtypeStruct((devices,) +...  30.6 us
    reshape x1, local copies, waits for them, and re-layouts, body(): field = probes.reshape(groups, LANES, nx, ny, nz).transpose(0, 2, 3, 1, 4)  11 us
    transpose x1, local copies, waits for them, and re-layouts, body(): fields = state.transpose(0, 3, 1, 2, 4).reshape(probes.shape)  9.26 us
    gather x1, local copies, waits for them, and re-layouts, body(): jnp.take(state.reshape(groups, nx * ny, LANES, nz), cells // nz, axis=1,...  4.06 us

commit v1 on v0

v1 whole, which is shorter than its diff:
```python
import math

import jax
import jax.numpy as jnp
from jax import lax
from jax.experimental import pallas as pl
from jax.experimental.pallas import tpu as pltpu
from jax.sharding import PartitionSpec as P

STEPS = 2
SWEEPS = 4

time_step = 2.0

LANES = 8
CHUNK = 8
TILE = 128
MESH = pl.DeviceIdType.MESH


def buffers(k):
    read = 0 if k == 0 else 2 - k % 2
    written = 0 if k == SWEEPS - 1 else 1 + k % 2
    return read, 0, written


def chips_in_row(n_gx):
    row = math.isqrt(max(n_gx // 2, 0))
    return row if row >= 2 and 2 * row * row == n_gx else 0


def unflatten(flat, columns):
    per = TILE // columns
    sub = lax.broadcasted_iota(jnp.int32, (per, TILE), 0)
    lane = lax.broadcasted_iota(jnp.int32, (per, TILE), 1)
    tiles = []
    for t in range(flat.shape[0]):
        wide = jnp.broadcast_to(flat[t : t + 1], (per, TILE))
        rows = wide
        for j in range(1, per):
            rows = jnp.where(sub == j, pltpu.roll(wide, TILE - columns * j, 1), rows)
        tiles.append(jnp.where(lane < columns, rows, 0.0))
    return jnp.concatenate(tiles, axis=0)


def flatten(rows, columns):
    per = TILE // columns
    sub = lax.broadcasted_iota(jnp.int32, (per, TILE), 0)
    tiles = []
    for t in range(rows.shape[0] // per):
        part = rows[t * per : (t + 1) * per]
        flat = jnp.where(sub == 0, part, 0.0)
        for j in range(1, per):
            flat = flat + jnp.where(sub == j, pltpu.roll(part, columns * j, 1), 0.0)
        tiles.append(jnp.sum(flat, axis=0, keepdims=True))
    return jnp.concatenate(tiles, axis=0)


def whole_kernel(
    wind_in, cells_in, count_in, field, diffusivity, weights_in, owners_in,
    state, goal_out, gram_out,
    held0, held1, held2, inv, mix, passing, contrib, landed, gram_mine, gram_landed, wind, cells, count, weights, owners,
    load_sem, small_sem, send_sem, recv_sem, pass_recv, pass_send, term_sem, gram_sem,
):
    held = (held0, held1, held2)
    groups, nx, ny = held0.shape[0], held0.shape[1] - 2, held0.shape[2] - 2
    nz = held0.shape[4]
    tiles = nz // TILE
    half = ny // 2
    gx, gy = lax.axis_index("gx"), lax.axis_index("gy")
    n_gx, n_gy = lax.axis_size("gx"), lax.axis_size("gy")
    devices = n_gx * n_gy
    me = gx * n_gy + gy
    xs, ys = pl.ds(1, nx), pl.ds(1, ny)
    row = chips_in_row(n_gx)

    def place(k):
        other = lax.rem(me + k, devices)
        return (lax.div(other, n_gy), lax.rem(other, n_gy))

    barrier = pltpu.get_barrier_semaphore()

    def greet(k, carry):
        pl.semaphore_signal(barrier, inc=1, device_id=place(k), device_id_type=MESH)
        return carry

    lax.fori_loop(1, devices, greet, 0)

    small = [
        pltpu.make_async_copy(src, dst, small_sem.at[i])
        for i, (src, dst) in enumerate(
            ((wind_in, wind), (cells_in, cells), (count_in, count), (weights_in, weights), (owners_in, owners))
        )
    ]
    small[0].start()

    def load(part, p):
        where = (pl.ds(0, 1), pl.ds(nx - 1, 1), pl.ds(1, nx - 2))[part]
        land = (pl.ds(1, 1), pl.ds(nx, 1), pl.ds(2, nx - 2))[part]
        return pltpu.make_async_copy(
            field.at[p, where],
            held0.at[p // LANES, land, ys, p % LANES],
            load_sem.at[part, p],
        )

    probes = groups * LANES
    for p in range(probes):
        load(0, p).start()
        load(1, p).start()
    for p in range(LANES):
        load(2, p).start()
    coefficient = pltpu.make_async_copy(diffusivity, mix, load_sem.at[3, 0])
    coefficient.start()
    for p in range(LANES, probes):
        load(2, p).start()
    for copy in small[1:]:
        copy.start()

    has_up, has_down = gx < n_gx - 1, gx > 0
    has_next, has_back = gy < n_gy - 1, gy > 0
    blank_x = jnp.zeros((ny, LANES, nz), jnp.float32)
    blank_y = jnp.zeros((nx, LANES, nz), jnp.float32)

    @pl.when(jnp.logical_not(has_down))
    def _():
        for b in range(3):
            for g in range(groups):
                held[b][g, 0, ys] = blank_x

    @pl.when(jnp.logical_not(has_up))
    def _():
        for b in range(3):
            for g in range(groups):
                held[b][g, nx + 1, ys] = blank_x

    @pl.when(jnp.logical_not(has_back))
    def _():
        for b in range(3):
            for g in range(groups):
                held[b][g, xs, 0] = blank_y

    @pl.when(jnp.logical_not(has_next))
    def _():
        for b in range(3):
            for g in range(groups):
                held[b][g, xs, ny + 1] = blank_y

    pl.semaphore_wait(barrier, devices - 1)

    if row:
        wide = 2 * row
        far_up = jnp.logical_and(has_up, lax.rem(gx, wide) == wide - 1)
        far_down = jnp.logical_and(has_down, lax.rem(gx, wide) == 0)
        passes = (
            jnp.logical_and(gx >= wide, lax.rem(gx, wide) == wide - 1),
            jnp.logical_and(gx < n_gx - wide, lax.rem(gx, wide) == 0),
        )
        pass_from = ((gx + wide, gy), (gx - wide, gy))
        pass_to = ((gx - wide + 1, gy), (gx + wide - 1, gy))
        near_up = jnp.logical_and(has_up, lax.rem(gx, wide) != wide - 1)
        near_down = jnp.logical_and(has_down, lax.rem(gx, wide) != 0)
    else:
        near_up, near_down = has_up, has_down

    routes = ((gx + 1, gy), (gx - 1, gy), (gx, gy + 1), (gx, gy - 1))
    sends = (has_up, has_up, has_down, has_down, has_next, has_back)
    receives = (has_down, has_down, has_up, has_up, has_back, has_next)

    def face(d, b, g, turn):
        if d < 4:
            rows = pl.ds(1 + (d % 2) * half, half)
            if d < 2:
                src, dst, target = held[b].at[g, nx, rows], held[b].at[g, 0, rows], routes[0]
            else:
                src, dst, target = held[b].at[g, 1, rows], held[b].at[g, nx + 1, rows], routes[1]
        elif d == 4:
            src, dst, target = held[b].at[g, xs, ny], held[b].at[g, xs, 0], routes[2]
        else:
            src, dst, target = held[b].at[g, xs, 1], held[b].at[g, xs, ny + 1], routes[3]
        return pltpu.make_async_remote_copy(
            src_ref=src,
            dst_ref=dst,
            send_sem=send_sem.at[turn % 2, g, d],
            recv_sem=recv_sem.at[turn % 2, g, d],
            device_id=target,
            device_id_type=MESH,
        )

    def detour(way, b, g, turn):
        rows = pl.ds(1 + half, half)
        return pltpu.make_async_remote_copy(
            src_ref=held[b].at[g, (nx, 1)[way], rows],
            dst_ref=passing.at[turn, g],
            send_sem=send_sem.at[turn % 2, g, 2 * way + 1],
            recv_sem=pass_recv.at[turn, g],
            device_id=pass_from[way],
            device_id_type=MESH,
        )

    def onward(way, b, g, turn):
        rows = pl.ds(1 + half, half)
        return pltpu.make_async_remote_copy(
            src_ref=passing.at[turn, g],
            dst_ref=held[b].at[g, (0, nx + 1)[way], rows],
            send_sem=pass_send.at[turn, g],
            recv_sem=recv_sem.at[turn % 2, g, 2 * way + 1],
            device_id=pass_to[way],
            device_id_type=MESH,
        )

    def start(d, b, g, turn):
        @pl.when((near_up, near_down)[d // 2] if d in (1, 3) else sends[d])
        def _():
            face(d, b, g, turn).start()

        if row and d in (1, 3):
            @pl.when((far_up, far_down)[d // 2])
            def _():
                detour(d // 2, b, g, turn).start()

    def start_x(b, g, turn):
        for d in (1, 3, 0, 2):
            start(d, b, g, turn)

    def start_y(b, g, turn):
        for d in (4, 5):
            start(d, b, g, turn)

    def wait_sends(b, g, turn):
        for d in range(6):
            @pl.when(sends[d])
            def _():
                face(d, b, g, turn).wait_send()

    def wait_recv(ways, b, g, turn):
        for d in ways:
            @pl.when(receives[d])
            def _():
                face(d, b, g, turn).wait_recv()

    def pass_on(b, g, turn):
        if row:
            for way in (0, 1):
                @pl.when(passes[way])
                def _():
                    detour(way, b, g, turn).wait_recv()
                    onward(way, b, g, turn).start()

    def pass_done(b, g, turn):
        if row:
            for way in (0, 1):
                @pl.when(passes[way])
                def _():
                    onward(way, b, g, turn).wait_send()

    for g in range(groups):
        for p in range(g * LANES, (g + 1) * LANES):
            load(0, p).wait()
            load(1, p).wait()
        start_x(0, g, 0)

    small[0].wait()
    w0, w1, w2 = time_step * wind[0], time_step * wind[1], time_step * wind[2]
    total_wind = wind[0] + wind[1] + wind[2]

    def coefficients(x, carry):
        a = mix[x]
        r = 1.0 / (1.0 + time_step * (6.0 * a + total_wind))
        inv[x] = jnp.where(a > 0.0, r, 0.0)
        mix[x] = jnp.where(a > 0.0, time_step * a * r, 0.0)
        return carry

    for g in range(groups):
        for p in range(g * LANES, (g + 1) * LANES):
            load(2, p).wait()
        start_y(0, g, 0)
        if g == 0:
            coefficient.wait()
            lax.fori_loop(0, nx, coefficients, 0)
    for g in range(groups):
        pass_on(0, g, 0)

    lane = lax.broadcasted_iota(jnp.int32, (LANES, TILE), 1)
    first, last_lane = lane == 0, lane == TILE - 1
    zero = jnp.zeros((LANES, TILE), jnp.float32)

    def plane(x, g, read, source, put):
        def tile(b, x, y, t):
            return held[b][g, x, y, :, t * TILE : (t + 1) * TILE]

        low = [tile(read, x, 0, t) for t in range(tiles)]
        centre = [tile(read, x, 1, t) for t in range(tiles)]
        for y in range(1, ny + 1):
            i, k = divmod(y - 1, CHUNK)
            high = [tile(read, x, y + 1, t) for t in range(tiles)]
            down = [pltpu.roll(c, 1, 1) for c in centre]
            up = [pltpu.roll(c, TILE - 1, 1) for c in centre]
            for t in range(tiles):
                cols = slice(t * TILE, (t + 1) * TILE)
                z_low = lax.select(first, down[t - 1] if t else zero, down[t])
                z_high = lax.select(last_lane, up[t + 1] if t + 1 < tiles else zero, up[t])
                x_low = tile(read, x - 1, y, t)
                x_high = tile(read, x + 1, y, t)
                beside = (x_low + x_high) + (low[t] + high[t]) + (z_low + z_high)
                upwind = w0 * x_low + w1 * low[t] + w2 * z_low
                begun = tile(source, x, y, t)
                r = jnp.broadcast_to(inv[x - 1, i, k : k + 1, cols], (LANES, TILE))
                a = jnp.broadcast_to(mix[x - 1, i, k : k + 1, cols], (LANES, TILE))
                put(g, x, y, cols, (begun + upwind) * r + a * beside)
            low, centre = centre, high

    total = STEPS * SWEEPS

    def sweep(step, k, last=False):
        read, source, written = buffers(k)
        turn = step * SWEEPS + k
        if last:
            def put(g, x, y, cols, value):
                state[g, x - 1, y - 1, :, cols] = value
        else:
            def put(g, x, y, cols, value):
                held[written][g, x, y, :, cols] = value

        def group(g, carry):
            def end(i, carry):
                plane(1 + i * (nx - 1), g, read, source, put)
                return carry

            def inner(x, carry):
                plane(x, g, read, source, put)
                return carry

            @pl.when(turn >= 1)
            def _():
                wait_sends(read, g, turn - 1)

            wait_recv((4, 5), read, g, turn)
            if last:
                lax.fori_loop(2, nx, inner, 0)
            wait_recv((0, 1, 2, 3), read, g, turn)
            lax.fori_loop(0, 2, end, 0)
            if not last:
                start_x(written, g, turn + 1)
                lax.fori_loop(2, nx, inner, 0)
                start_y(written, g, turn + 1)
                pass_on(written, g, turn + 1)
            return carry

        lax.fori_loop(0, groups, group, 0)

    def one_step(step, carry):
        for k in range(SWEEPS - 1):
            sweep(step, k)

        @pl.when(step < STEPS - 1)
        def _():
            sweep(step, SWEEPS - 1)

        return carry

    lax.fori_loop(0, STEPS, one_step, 0)
    sweep(STEPS - 1, SWEEPS - 1, True)
    for g in range(groups):
        wait_sends(0, g, total - 1)
        lax.fori_loop(0, total, lambda turn, carry: pass_done(0, g, turn) or carry, 0)
    for copy in small[1:]:
        copy.wait()

    sensors = cells.shape[0]

    column_of = lax.broadcasted_iota(jnp.int32, (LANES, nz), 1)
    unroll = math.gcd(sensors, 32)

    def look(i, carry):
        acc = list(carry)
        for k in range(unroll):
            s = i * unroll + k
            cell = cells[s]
            column = lax.div(cell, nz)
            hit = column_of == lax.rem(cell, nz)
            for g in range(groups):
                value = lax.select(hit, state[g, lax.div(column, ny), lax.rem(column, ny)], jnp.zeros((LANES, nz), jnp.float32))
                acc[g] = jnp.where(lane == s, jnp.sum(value, axis=1, keepdims=True), acc[g])
        return tuple(acc)

    readings = jnp.concatenate(lax.fori_loop(0, sensors // unroll, look, (zero,) * groups), axis=0)
    active = lax.broadcasted_iota(jnp.int32, (probes, sensors), 1) < count[0]
    readings = jnp.where(active, readings, 0.0)
    weight = weights[...]
    goal_count = weight.shape[0]
    outer = (weight[:, None, :] * readings[None, :, :]).reshape(goal_count * probes, sensors)
    onehot = (
        lax.broadcasted_iota(jnp.int32, (devices, sensors), 0) == jnp.broadcast_to(owners[...], (devices, sensors))
    ).astype(jnp.float32)
    terms = lax.dot_general(
        onehot, outer, (((1,), (1,)), ((), ())),
        precision=lax.Precision.HIGHEST, preferred_element_type=jnp.float32,
    )
    spans = contrib.shape[1]
    for t in range(spans):
        contrib[:, t, :] = terms[:, t * TILE : (t + 1) * TILE]

    def exchange(source, into, sem):
        def copy(k, slot):
            return pltpu.make_async_remote_copy(
                src_ref=source(k),
                dst_ref=into.at[slot],
                send_sem=sem.at[0, k],
                recv_sem=sem.at[1, k],
                device_id=place(k),
                device_id_type=MESH,
            )

        def send(k, carry):
            copy(k, me).start()
            return carry

        def finish(k, carry):
            arriving = copy(k, lax.rem(me + devices - k, devices))
            arriving.wait_send()
            arriving.wait_recv()
            return carry

        lax.fori_loop(1, devices, send, 0)
        into[pl.ds(me, 1)] = source(0)[...][None]
        lax.fori_loop(1, devices, finish, 0)
        return jnp.sum(into[...], axis=0)

    goal = exchange(lambda k: contrib.at[lax.rem(me + k, devices)], landed, term_sem)
    goal = unflatten(goal, probes)
    goal_out[...] = goal[:, :probes]
    gram = jnp.dot(
        goal.T[:probes], goal, precision=lax.Precision.HIGHEST, preferred_element_type=jnp.float32
    )
    gram_mine[...] = flatten(gram, probes)
    gram = exchange(lambda k: gram_mine, gram_landed, gram_sem)
    gram_out[...] = unflatten(gram, probes)[:, :probes]


def store_kernel(state, goal, gram, out, goal_out, gram_out, store_sem, small_sem):
    copies = [
        pltpu.make_async_copy(state.at[p // LANES, :, :, p % LANES], out.at[p], store_sem.at[p])
        for p in range(out.shape[0])
    ]
    copies.append(pltpu.make_async_copy(goal, goal_out, small_sem.at[0]))
    copies.append(pltpu.make_async_copy(gram, gram_out, small_sem.at[1]))
    for copy in copies:
        copy.start()
    for copy in copies:
        copy.wait()


def body(probes, diffusivity, wind_speed, sensor_cell, sensor_owner, sensor_count, goal_weight):
    probe_count, nx, ny, nz = probes.shape
    groups = probe_count // LANES
    sensors, goal_count = sensor_cell.shape[2], goal_weight.shape[3]
    devices = lax.axis_size("gx") * lax.axis_size("gy")
    spans = goal_count * probe_count // TILE
    gram_spans = probe_count * probe_count // TILE
    f32 = jnp.float32
    hbm = pl.BlockSpec(memory_space=pltpu.HBM)
    smem = pl.BlockSpec(memory_space=pltpu.SMEM)
    vmem = pl.BlockSpec(memory_space=pltpu.VMEM)
    results = (
        jax.ShapeDtypeStruct((groups, nx, ny, LANES, nz), f32),
        jax.ShapeDtypeStruct((goal_count, probe_count), f32),
        jax.ShapeDtypeStruct((probe_count, probe_count), f32),
    )
    state, goal, gram = pl.pallas_call(
        whole_kernel,
        out_shape=tuple(pltpu.VMEM(r.shape, r.dtype) for r in results),
        in_specs=[hbm] * 7,
        out_specs=(vmem, vmem, vmem),
        scratch_shapes=[
            *[pltpu.VMEM((groups, nx + 2, ny + 2, LANES, nz), f32)] * 3,
            pltpu.VMEM((nx, ny // CHUNK, CHUNK, nz), f32),
            pltpu.VMEM((nx, ny // CHUNK, CHUNK, nz), f32),
            pltpu.VMEM((STEPS * SWEEPS, groups, ny // 2, LANES, nz), f32),
            pltpu.VMEM((devices, spans, TILE), f32),
            pltpu.VMEM((devices, spans, TILE), f32),
            pltpu.VMEM((gram_spans, TILE), f32),
            pltpu.VMEM((devices, gram_spans, TILE), f32),
            pltpu.SMEM((3,), f32),
            pltpu.SMEM((sensors,), jnp.int32),
            pltpu.SMEM((1,), jnp.int32),
            pltpu.VMEM((goal_count, sensors), f32),
            pltpu.VMEM((1, sensors), jnp.int32),
            pltpu.SemaphoreType.DMA((4, probe_count)),
            pltpu.SemaphoreType.DMA((5,)),
            pltpu.SemaphoreType.DMA((2, groups, 6)),
            pltpu.SemaphoreType.DMA((2, groups, 6)),
            pltpu.SemaphoreType.DMA((STEPS * SWEEPS, groups)),
            pltpu.SemaphoreType.DMA((STEPS * SWEEPS, groups)),
            pltpu.SemaphoreType.DMA((2, devices)),
            pltpu.SemaphoreType.DMA((2, devices)),
        ],
        compiler_params=pltpu.CompilerParams(
            collective_id=0, has_side_effects=True, vmem_limit_bytes=40 * 1024 * 1024
        ),
    )(
        pltpu.with_memory_space_constraint(wind_speed, pltpu.HBM),
        pltpu.with_memory_space_constraint(sensor_cell.reshape(sensors), pltpu.HBM),
        sensor_count.reshape(1),
        pltpu.with_memory_space_constraint(probes, pltpu.HBM),
        pltpu.with_memory_space_constraint(diffusivity.reshape(nx, ny // CHUNK, CHUNK, nz), pltpu.HBM),
        pltpu.with_memory_space_constraint(goal_weight.reshape(sensors, goal_count).T, pltpu.HBM),
        pltpu.with_memory_space_constraint(sensor_owner.reshape(1, sensors), pltpu.HBM),
    )
    return pl.pallas_call(
        store_kernel,
        out_shape=(jax.ShapeDtypeStruct(probes.shape, f32), *results[1:]),
        in_specs=[vmem] * 3,
        out_specs=(hbm, hbm, hbm),
        scratch_shapes=[pltpu.SemaphoreType.DMA((probe_count,)), pltpu.SemaphoreType.DMA((2,))],
        compiler_params=pltpu.CompilerParams(has_side_effects=True, vmem_limit_bytes=1024 * 1024),
    )(state, goal, gram)


def solution(mesh):
    placed = (
        P(None, "gx", "gy", None),
        P("gx", "gy", None),
        P(),
        P("gx", "gy", None),
        P("gx", "gy", None, None),
        P("gx", "gy"),
        P("gx", "gy", None, None),
    )
    return jax.shard_map(
        body,
        mesh=mesh,
        in_specs=placed,
        out_specs=(P(None, "gx", "gy", None), P(("gx", "gy"), None), P()),
        check_vma=False,
    )
```

time: 168 us -> 104 us (0.62)
  local copies, waits for them, and re-layouts: 34.6 us -> 0 us
  Pallas kernels: 124 us -> 102 us
  other arithmetic: 4.75 us -> 0 us
  matrix products: 3.36 us -> 0 us
    pallas_call x2, Pallas kernels: 124 us -> 102 us  [the longest x1 98.8 us: body(): pl.pallas_call(whole_kernel, out_shape=tuple((pltpu.VMEM(r.shape, r.dtype...]
    reshape x3 -> x0, local copies, waits for them, and re-layouts: 12.2 us -> none  [the longest x1 11 us: body(): field = probes.reshape(groups, LANES, nx, ny, nz).transpose(0, 2, 3, 1, 4)]
    transpose x1 -> x0, local copies, waits for them, and re-layouts: 9.26 us -> none  [body(): fields = state.transpose(0, 3, 1, 2, 4).reshape(probes.shape)]
    broadcast_in_dim x2 -> x0, local copies, waits for them, and re-layouts: 4.86 us -> none  [the longest x1 2.43 us: body(): jnp.broadcast_to(inverse[:, :, None, :], wide)]
    mul x3 -> x0, other arithmetic: 4.12 us -> none  [the longest x1 3.15 us: body(): mixing = time_step * diffusivity * inverse]
    gather x1 -> x0, local copies, waits for them, and re-layouts: 4.06 us -> none  [body(): jnp.take(state.reshape(groups, nx * ny, LANES, nz), cells // nz, axis=1,...]
    dot_general x2 -> x0, matrix products: 3.36 us -> none  [the longest x1 2.2 us: body(): goals = jnp.dot(onehot.T, outer, precision=lax.Precision.HIGHEST)]
where the time goes in v1:
time: 104 us
  Pallas kernels  102 us (98%)
  between operations  1.29 us (1%)
    pallas_call x1, Pallas kernels, body(): pl.pallas_call(whole_kernel, out_shape=tuple((pltpu.VMEM(r.shape, r.dtype...  98.8 us
    pallas_call x1, Pallas kernels, body(): pl.pallas_call(store_kernel, out_shape=(jax.ShapeDtypeStruct(probes.shape...  3.44 us

profile of v1, /device:TPU:0, one launch (start us, length us, event | category | flops | bytes accessed | tf_op | source)
XLA Modules:
  0.0 103.5 jit_solution(11061194154974631948)
XLA Ops:
  1.3 98.8 %shard_map.94 = (f32[2,16,32,8,256]{4,3,2,1,0:T(8,128)S(1)}, f32[16,16]{1,0:T(8,128)S(1)}, f32[16,16]{1,0:T(8,128)S(1)}) custom-call(f32[3]{0:T(128)} %wind_in.1, s32[128]{0:T(128)} %bitcast.10, s32[1]{0:T(128)} %bitcast.7.count_in, f32[16,16,32,256]{3,2,1,0:T(8,128)} %field.1, f32[16,4,8,256]{3,2,1,0:T(8,128)} %bitcast.8, f32[16,128]{1,0:T(8,128)} %bitcast.9, ...), custom_call_target="tpu_custom_call" | custom-call | tf_op jit(solution)/shard_map/pallas_call | solution.py:469
  100.1 3.4 %shard_map.95 = (f32[16,16,32,256]{3,2,1,0:T(8,128)}, f32[16,16]{1,0:T(8,128)}, f32[16,16]{1,0:T(8,128)}) custom-call(f32[2,16,32,8,256]{4,3,2,1,0:T(8,128)S(1)} %get-tuple-element.6.state, f32[16,16]{1,0:T(8,128)S(1)} %get-tuple-element.7.goal, f32[16,16]{1,0:T(8,128)S(1)} %get-tuple-element.8.gram), custom_call_target="tpu_custom_call" | custom-call | tf_op jit(solution)/shard_map/pallas_call | solution.py:509

commit v2 on v1

--- a/solution.py
+++ b/solution.py
@@ -14,6 +14,7 @@
 
 LANES = 8
 CHUNK = 8
+DETOUR = 8
 TILE = 128
 MESH = pl.DeviceIdType.MESH
 
@@ -66,7 +67,8 @@
     groups, nx, ny = held0.shape[0], held0.shape[1] - 2, held0.shape[2] - 2
     nz = held0.shape[4]
     tiles = nz // TILE
-    half = ny // 2
+    part = passing.shape[3]
+    pieces = (pl.ds(1, ny - 2 * part), pl.ds(1 + ny - 2 * part, part), pl.ds(1 + ny - part, part))
     gx, gy = lax.axis_index("gx"), lax.axis_index("gy")
     n_gx, n_gy = lax.axis_size("gx"), lax.axis_size("gy")
     devices = n_gx * n_gy
@@ -163,17 +165,16 @@
         near_up, near_down = has_up, has_down
 
     routes = ((gx + 1, gy), (gx - 1, gy), (gx, gy + 1), (gx, gy - 1))
-    sends = (has_up, has_up, has_down, has_down, has_next, has_back)
-    receives = (has_down, has_down, has_up, has_up, has_back, has_next)
+    sends = (has_up,) * 3 + (has_down,) * 3 + (has_next, has_back)
+    receives = (has_down,) * 3 + (has_up,) * 3 + (has_back, has_next)
+    UP, DOWN, SIDE = (1, 2, 0), (4, 5, 3), (6, 7)
 
     def face(d, b, g, turn):
-        if d < 4:
-            rows = pl.ds(1 + (d % 2) * half, half)
-            if d < 2:
-                src, dst, target = held[b].at[g, nx, rows], held[b].at[g, 0, rows], routes[0]
-            else:
-                src, dst, target = held[b].at[g, 1, rows], held[b].at[g, nx + 1, rows], routes[1]
-        elif d == 4:
+        if d < 3:
+            src, dst, target = held[b].at[g, nx, pieces[d]], held[b].at[g, 0, pieces[d]], routes[0]
+        elif d < 6:
+            src, dst, target = held[b].at[g, 1, pieces[d - 3]], held[b].at[g, nx + 1, pieces[d - 3]], routes[1]
+        elif d == 6:
             src, dst, target = held[b].at[g, xs, ny], held[b].at[g, xs, 0], routes[2]
         else:
             src, dst, target = held[b].at[g, xs, 1], held[b].at[g, xs, ny + 1], routes[3]
@@ -186,48 +187,40 @@
             device_id_type=MESH,
         )
 
-    def detour(way, b, g, turn):
-        rows = pl.ds(1 + half, half)
+    def detour(way, c, b, g, turn):
         return pltpu.make_async_remote_copy(
-            src_ref=held[b].at[g, (nx, 1)[way], rows],
-            dst_ref=passing.at[turn, g],
-            send_sem=send_sem.at[turn % 2, g, 2 * way + 1],
-            recv_sem=pass_recv.at[turn, g],
+            src_ref=held[b].at[g, (nx, 1)[way], pieces[c]],
+            dst_ref=passing.at[turn, g, c - 1],
+            send_sem=send_sem.at[turn % 2, g, 3 * way + c],
+            recv_sem=pass_recv.at[turn, g, c - 1],
             device_id=pass_from[way],
             device_id_type=MESH,
         )
 
-    def onward(way, b, g, turn):
-        rows = pl.ds(1 + half, half)
+    def onward(way, c, b, g, turn):
         return pltpu.make_async_remote_copy(
-            src_ref=passing.at[turn, g],
-            dst_ref=held[b].at[g, (0, nx + 1)[way], rows],
-            send_sem=pass_send.at[turn, g],
-            recv_sem=recv_sem.at[turn % 2, g, 2 * way + 1],
+            src_ref=passing.at[turn, g, c - 1],
+            dst_ref=held[b].at[g, (0, nx + 1)[way], pieces[c]],
+            send_sem=pass_send.at[turn, g, c - 1],
+            recv_sem=recv_sem.at[turn % 2, g, 3 * way + c],
             device_id=pass_to[way],
             device_id_type=MESH,
         )
 
-    def start(d, b, g, turn):
-        @pl.when((near_up, near_down)[d // 2] if d in (1, 3) else sends[d])
-        def _():
-            face(d, b, g, turn).start()
-
-        if row and d in (1, 3):
-            @pl.when((far_up, far_down)[d // 2])
+    def start(ways, b, g, turn):
+        for d in ways:
+            passed = row and d in (1, 2, 4, 5)
+            @pl.when((near_up, near_down)[d // 3] if passed else sends[d])
             def _():
-                detour(d // 2, b, g, turn).start()
-
-    def start_x(b, g, turn):
-        for d in (1, 3, 0, 2):
-            start(d, b, g, turn)
-
-    def start_y(b, g, turn):
-        for d in (4, 5):
-            start(d, b, g, turn)
+                face(d, b, g, turn).start()
+
+            if passed:
+                @pl.when((far_up, far_down)[d // 3])
+                def _():
+                    detour(d // 3, d % 3, b, g, turn).start()
 
     def wait_sends(b, g, turn):
-        for d in range(6):
+        for d in range(8):
             @pl.when(sends[d])
             def _():
                 face(d, b, g, turn).wait_send()
@@ -243,21 +236,23 @@
             for way in (0, 1):
                 @pl.when(passes[way])
                 def _():
-                    detour(way, b, g, turn).wait_recv()
-                    onward(way, b, g, turn).start()
-
-    def pass_done(b, g, turn):
+                    for c in (1, 2):
+                        detour(way, c, b, g, turn).wait_recv()
+                        onward(way, c, b, g, turn).start()
+
+    def pass_done(g, turn):
         if row:
             for way in (0, 1):
                 @pl.when(passes[way])
                 def _():
-                    onward(way, b, g, turn).wait_send()
+                    for c in (1, 2):
+                        onward(way, c, 0, g, turn).wait_send()
 
     for g in range(groups):
         for p in range(g * LANES, (g + 1) * LANES):
             load(0, p).wait()
             load(1, p).wait()
-        start_x(0, g, 0)
+        start(UP + DOWN, 0, g, 0)
 
     small[0].wait()
     w0, w1, w2 = time_step * wind[0], time_step * wind[1], time_step * wind[2]
@@ -273,7 +268,7 @@
     for g in range(groups):
         for p in range(g * LANES, (g + 1) * LANES):
             load(2, p).wait()
-        start_y(0, g, 0)
+        start(SIDE, 0, g, 0)
         if g == 0:
             coefficient.wait()
             lax.fori_loop(0, nx, coefficients, 0)
@@ -284,13 +279,13 @@
     first, last_lane = lane == 0, lane == TILE - 1
     zero = jnp.zeros((LANES, TILE), jnp.float32)
 
-    def plane(x, g, read, source, put):
+    def plane(x, g, read, source, put, begin, end):
         def tile(b, x, y, t):
             return held[b][g, x, y, :, t * TILE : (t + 1) * TILE]
 
-        low = [tile(read, x, 0, t) for t in range(tiles)]
-        centre = [tile(read, x, 1, t) for t in range(tiles)]
-        for y in range(1, ny + 1):
+        low = [tile(read, x, begin - 1, t) for t in range(tiles)]
+        centre = [tile(read, x, begin, t) for t in range(tiles)]
+        for y in range(begin, end):
             i, k = divmod(y - 1, CHUNK)
             high = [tile(read, x, y + 1, t) for t in range(tiles)]
             down = [pltpu.roll(c, 1, 1) for c in centre]
@@ -323,26 +318,43 @@
 
         def group(g, carry):
             def end(i, carry):
-                plane(1 + i * (nx - 1), g, read, source, put)
+                side = lax.rem(gx + i, 2)
+
+                @pl.when(side == 1)
+                def _():
+                    wait_recv(DOWN, read, g, turn)
+
+                @pl.when(side == 0)
+                def _():
+                    wait_recv(UP, read, g, turn)
+
+                plane(1 + side * (nx - 1), g, read, source, put, 1, ny + 1)
+                if not last:
+                    @pl.when(side == 1)
+                    def _():
+                        start(UP, written, g, turn + 1)
+
+                    @pl.when(side == 0)
+                    def _():
+                        start(DOWN, written, g, turn + 1)
+
                 return carry
 
             def inner(x, carry):
-                plane(x, g, read, source, put)
+                plane(x, g, read, source, put, 1, ny + 1)
                 return carry
 
             @pl.when(turn >= 1)
             def _():
                 wait_sends(read, g, turn - 1)
 
-            wait_recv((4, 5), read, g, turn)
+            wait_recv(SIDE, read, g, turn)
             if last:
                 lax.fori_loop(2, nx, inner, 0)
-            wait_recv((0, 1, 2, 3), read, g, turn)
             lax.fori_loop(0, 2, end, 0)
             if not last:
-                start_x(written, g, turn + 1)
-                lax.fori_loop(2, nx, inner, 0)
-                start_y(written, g, turn + 1)
+                lax.fori_loop(2, nx, inner, 0, unroll=2)
+                start(SIDE, written, g, turn + 1)
                 pass_on(written, g, turn + 1)
             return carry
 
@@ -362,7 +374,7 @@
     sweep(STEPS - 1, SWEEPS - 1, True)
     for g in range(groups):
         wait_sends(0, g, total - 1)
-        lax.fori_loop(0, total, lambda turn, carry: pass_done(0, g, turn) or carry, 0)
+        lax.fori_loop(0, total, lambda turn, carry: pass_done(g, turn) or carry, 0)
     for copy in small[1:]:
         copy.wait()
 
@@ -475,7 +487,7 @@
             *[pltpu.VMEM((groups, nx + 2, ny + 2, LANES, nz), f32)] * 3,
             pltpu.VMEM((nx, ny // CHUNK, CHUNK, nz), f32),
             pltpu.VMEM((nx, ny // CHUNK, CHUNK, nz), f32),
-            pltpu.VMEM((STEPS * SWEEPS, groups, ny // 2, LANES, nz), f32),
+            pltpu.VMEM((STEPS * SWEEPS, groups, 2, ny * DETOUR // 32, LANES, nz), f32),
             pltpu.VMEM((devices, spans, TILE), f32),
             pltpu.VMEM((devices, spans, TILE), f32),
             pltpu.VMEM((gram_spans, TILE), f32),
@@ -487,10 +499,10 @@
             pltpu.VMEM((1, sensors), jnp.int32),
             pltpu.SemaphoreType.DMA((4, probe_count)),
             pltpu.SemaphoreType.DMA((5,)),
-            pltpu.SemaphoreType.DMA((2, groups, 6)),
-            pltpu.SemaphoreType.DMA((2, groups, 6)),
-            pltpu.SemaphoreType.DMA((STEPS * SWEEPS, groups)),
-            pltpu.SemaphoreType.DMA((STEPS * SWEEPS, groups)),
+            pltpu.SemaphoreType.DMA((2, groups, 8)),
+            pltpu.SemaphoreType.DMA((2, groups, 8)),
+            pltpu.SemaphoreType.DMA((STEPS * SWEEPS, groups, 2)),
+            pltpu.SemaphoreType.DMA((STEPS * SWEEPS, groups, 2)),
             pltpu.SemaphoreType.DMA((2, devices)),
             pltpu.SemaphoreType.DMA((2, devices)),
         ],

time: 104 us -> 98.4 us (0.946)
  Pallas kernels: 102 us -> 97 us
    pallas_call x1, Pallas kernels: 98.8 us -> 93.5 us  [body(): pl.pallas_call(whole_kernel, out_shape=tuple((pltpu.VMEM(r.shape, r.dtype...]
where the time goes in v2:
time: 98.4 us; the launch traced here: 98.2 us
  Pallas kernels  97 us (99%)
  between operations  1.29 us (1%)
    pallas_call x1, Pallas kernels, body(): pl.pallas_call(whole_kernel, out_shape=tuple((pltpu.VMEM(r.shape, r.dtype...  93.5 us
    pallas_call x1, Pallas kernels, body(): pl.pallas_call(store_kernel, out_shape=(jax.ShapeDtypeStruct(probes.shape...  3.44 us

profile of v2, /device:TPU:0, one launch (start us, length us, event | category | flops | bytes accessed | tf_op | source)
XLA Modules:
  0.0 98.2 jit_solution(17983781885194352330)
XLA Ops:
  1.3 93.5 %shard_map.94 = (f32[2,16,32,8,256]{4,3,2,1,0:T(8,128)S(1)}, f32[16,16]{1,0:T(8,128)S(1)}, f32[16,16]{1,0:T(8,128)S(1)}) custom-call(f32[3]{0:T(128)} %wind_in.1, s32[128]{0:T(128)} %bitcast.10, s32[1]{0:T(128)} %bitcast.7.count_in, f32[16,16,32,256]{3,2,1,0:T(8,128)} %field.1, f32[16,4,8,256]{3,2,1,0:T(8,128)} %bitcast.8, f32[16,128]{1,0:T(8,128)} %bitcast.9, ...), custom_call_target="tpu_custom_call" | custom-call | tf_op jit(solution)/shard_map/pallas_call | solution.py:481
  94.8 3.4 %shard_map.95 = (f32[16,16,32,256]{3,2,1,0:T(8,128)}, f32[16,16]{1,0:T(8,128)}, f32[16,16]{1,0:T(8,128)}) custom-call(f32[2,16,32,8,256]{4,3,2,1,0:T(8,128)S(1)} %get-tuple-element.6.state, f32[16,16]{1,0:T(8,128)S(1)} %get-tuple-element.7.goal, f32[16,16]{1,0:T(8,128)S(1)} %get-tuple-element.8.gram), custom_call_target="tpu_custom_call" | custom-call | tf_op jit(solution)/shard_map/pallas_call | solution.py:521
